TPU v7x, 32 devices: a whole 2x2x4 slice. The times are simulated.
32 devices in a mesh: fsdp: 8 (over z, x), tp: 4 (over y, core).
Axes of the slice: x: 2, y: 2, z: 4, core: 2. Of those that a mesh axis runs over, the one named last changes fastest.
Arguments:
- slopes_in: float32 [32, 128, 4096], P(None, 'fsdp', 'tp'), may hold values from -6 to 6
- moments_in: float32 [32, 128, 4096], P(None, 'fsdp', 'tp'), may hold values from -6 to 6
- weights_in: float32 [32, 128, 4096], P(None, 'fsdp', 'tp'), may hold values from -0.1875 to 0.1875
Outputs:
- new_weights: float32 [32, 128, 4096], P(None, 'fsdp', 'tp')
- new_momentum: float32 [32, 128, 4096], P(None, 'fsdp', 'tp')
All inputs are finite; a program needn't handle non-finite values.
Results may differ from a plain program's by a relative error of at most 0.00021.
Values sent between devices are 32-bit elements; how exact they have to be, the bound alone decides.
A program may use at most 128 MiB of HBM per device.

v0:
```python
import functools
import jax
import jax.numpy as jnp
from jax import lax
from jax.sharding import PartitionSpec as P

ITERS = 5
HIGH = lax.Precision.HIGHEST
hold_rate = 0.8
learn_rate = 1.0


def polynomial(gram):
    side = gram.shape[-1]
    eye = jnp.eye(side, dtype=gram.dtype)
    dot = functools.partial(jnp.einsum, "mij,mjk->mik", precision=HIGH)
    scale = lax.rsqrt(jnp.sum(gram * eye, axis=(1, 2), keepdims=True) + 1e-06)
    gram = gram * (scale * scale)
    total = None
    for step in range(ITERS):
        mixed = 3.4445 * eye - 4.775 * gram + 2.0315 * dot(gram, gram)
        total = mixed * scale if total is None else dot(mixed, total)
        if step < ITERS - 1:
            gram = dot(dot(mixed, gram), mixed)
    return total


def body(slopes_in, moments_in, weights_in):
    new_momentum = hold_rate * moments_in + slopes_in
    moved = lax.all_to_all(new_momentum, "fsdp", split_axis=0, concat_axis=1, tiled=True)
    gram = lax.psum(jnp.einsum("mik,mjk->mij", moved, moved, precision=HIGH), "tp")
    iterate = jnp.einsum("mij,mjk->mik", polynomial(gram), moved, precision=HIGH)
    back = lax.all_to_all(iterate, "fsdp", split_axis=1, concat_axis=0, tiled=True)
    new_weights = weights_in - learn_rate * back
    return (new_weights, new_momentum)


def solution(mesh):
    return jax.shard_map(
        body,
        mesh=mesh,
        in_specs=(P(None, "fsdp", "tp"), P(None, "fsdp", "tp"), P(None, "fsdp", "tp")),
        out_specs=(P(None, "fsdp", "tp"), P(None, "fsdp", "tp")),
        check_vma=False,
    )
```

profile of v0, /device:TPU:0, one launch (start us, length us, event | category | flops | bytes accessed | tf_op | source)
XLA Modules:
  0.0 175.6 jit_solution(531279541024470661)
XLA Ops:
  7.2 0.0 all-reduce.2.cloned.1.call-start
  7.2 2.7 %multiply_add_fusion = f32[32,16,1024]{2,1,0:T(8,128)S(1)} fusion(f32[32,16,1024]{2,1,0:T(8,128)} %param.3, f32[32,16,1024]{2,1,0:T(8,128)} %param.4), kind=kLoop, calls=%fused_computation.1 | loop fusion | flops 1048576 | bytes 6291456 | tf_op jit(solution)/shard_map/add | solution.py:29
  9.9 0.0 copy-start
  9.9 55.3 %all_to_all.36 = f32[32,16,1024]{2,1,0:T(8,128)S(1)} all-to-all(f32[32,16,1024]{2,1,0:T(8,128)S(1)} %multiply_add_fusion), channel_id=1, replica_groups=mesh['fsdp'=8,'tp'=4] {'fsdp'}, dimensions={0} | all-to-all | bytes 4194304 | tf_op jit(solution)/shard_map/all_to_all | solution.py:30
  65.2 0.0 copy-done
  65.2 0.1 copy.7
  65.3 2.8 %fusion.16 = f32[4,128,128]{2,1,0:T(8,128)} fusion(f32[4,128,1024]{2,1,0:T(8,128)S(1)} %bitcast.43), kind=kOutput, calls=%fused_computation.26 | convolution fusion | flops 805306368 | bytes 2359296 | tf_op jit(solution)/shard_map/mik,mjk->mij/dot_general | solution.py:31
  68.1 0.0 all-reduce.2.cloned.1.call-update
  68.2 31.4 %all-reduce.2.cloned.1.call-done = f32[4,128,128]{2,1,0:T(8,128)} async-done(((f32[4,128,128]{2,1,0:T(8,128)}), f32[4,128,128]{2,1,0:T(8,128)}) %all-reduce.2.cloned.1.call-update) | async-done | bytes 262160 | tf_op jit(solution)/shard_map/psum | solution.py:31
  99.6 1.1 multiply_reduce_fusion
  100.7 1.6 fusion.4
  102.3 1.4 fusion.8
  103.7 0.4 fusion.17
  104.1 0.4 fusion.3
  104.5 0.4 fusion.18
  104.9 0.4 fusion.5
  105.3 0.4 fusion.19
  105.7 0.4 fusion.2
  106.1 0.4 fusion.20
  106.5 0.4 fusion.24
  106.9 0.4 fusion.21
  107.3 0.4 fusion.1
  107.7 0.4 fusion.22
  108.1 0.4 fusion.25
  108.5 0.4 fusion.23
  108.9 0.4 fusion
  109.3 0.4 fusion.26
  109.7 1.9 %fusion.27 = f32[4,128,1024]{2,1,0:T(8,128)S(1)} fusion(f32[4,128,128]{2,1,0:T(8,128)S(1)} %fusion.26, f32[4,128,1024]{2,1,0:T(8,128)S(1)} %bitcast.44), kind=kOutput, calls=%fused_computation.37 | convolution fusion | flops 805306368 | bytes 4456448 | tf_op jit(solution)/shard_map/mij,mjk->mik/dot_general | solution.py:32
  111.6 1.4 copy.8
  113.0 52.5 %all_to_all.37 = f32[4,128,1024]{2,0,1:T(4,128)S(1)} all-to-all(f32[4,128,1024]{2,0,1:T(4,128)S(1)} %copy.8), channel_id=1, replica_groups=mesh['fsdp'=8,'tp'=4] {'fsdp'}, dimensions={1} | all-to-all | bytes 4194304 | tf_op jit(solution)/shard_map/all_to_all | solution.py:33
  165.4 0.0 copy-start.1
  165.4 1.2 copy.9
  166.6 0.4 copy-done.1
  167.0 1.7 bitcast_subtract_fusion
  (3 shorter events, 0.0 us)
Async XLA Ops:
  7.2 92.4 %all-reduce.2.cloned.1.call-start = ((), (), s32[]{:S(2)}) async-start(), calls=%async_computation.2 | async-start | bytes 524288 | tf_op jit(solution)/shard_map/psum | solution.py:31
  9.9 55.3 %copy-start = (f32[32,16,1024]{2,1,0:T(8,128)}, f32[32,16,1024]{2,1,0:T(8,128)S(1)}, u32[]{:S(2)}) copy-start(f32[32,16,1024]{2,1,0:T(8,128)S(1)} %multiply_add_fusion) | copy-start | bytes 6291460
  165.4 1.6 copy-start.1
Sparse Core Ops, SparseCore 0:
  68.2 31.3 all-reduce.1
where the time goes:
time: 176 us
  blocking collectives  108 us (61%)
  waiting for transfers between devices  31.5 us (18%)
  between operations  14.2 us (8%)
  matrix products  13.5 us (8%)
  other arithmetic  5.5 us (3%)
  local copies, waits for them, and re-layouts  3.08 us (2%)
    all_to_all x1, blocking collectives, body(): lax.all_to_all(new_momentum, 'fsdp', split_axis=0, concat_axis=1, tiled=T...  55.3 us
    all_to_all x1, blocking collectives, body(): lax.all_to_all(iterate, 'fsdp', split_axis=1, concat_axis=0, tiled=True)  52.5 us
    psum x1, waiting for transfers between devices, body(): lax.psum(jnp.einsum('mik,mjk->mij', moved, moved, precision=HIGH), 'tp')  31.4 us
    dot_general x8, matrix products, polynomial(): gram = dot(dot(mixed, gram), mixed)  4.15 us
  transfers between devices with their start and end apart: 1, of which 1 were waited for; matrix products, arithmetic and copies ran while one was open for 0% of the time, Pallas kernels for 0%

commit v1 on v0

--- a/solution.py
+++ b/solution.py
@@ -28,7 +28,9 @@
 def body(slopes_in, moments_in, weights_in):
     new_momentum = hold_rate * moments_in + slopes_in
     moved = lax.all_to_all(new_momentum, "fsdp", split_axis=0, concat_axis=1, tiled=True)
-    gram = lax.psum(jnp.einsum("mik,mjk->mij", moved, moved, precision=HIGH), "tp")
+    gram = jnp.sum(
+        lax.all_gather(jnp.einsum("mik,mjk->mij", moved, moved, precision=HIGH), "tp"), axis=0
+    )
     iterate = jnp.einsum("mij,mjk->mik", polynomial(gram), moved, precision=HIGH)
     back = lax.all_to_all(iterate, "fsdp", split_axis=1, concat_axis=0, tiled=True)
     new_weights = weights_in - learn_rate * back

time: 176 us -> 160 us (0.909)
  waiting for transfers between devices: 31.5 us -> 15.9 us
  matrix products: 13.5 us -> 11.5 us
    psum x1 -> x0, waiting for transfers between devices: 31.4 us -> none  [body(): lax.psum(jnp.einsum('mik,mjk->mij', moved, moved, precision=HIGH), 'tp')]
    all_gather x0 -> x1, waiting for transfers between devices: none -> 15.9 us  [body(): lax.all_gather(jnp.einsum('mik,mjk->mij', moved, moved, precision=HIGH),...]
where the time goes in v1:
time: 160 us
  blocking collectives  109 us (68%)
  waiting for transfers between devices  15.9 us (10%)
  between operations  14.2 us (9%)
  matrix products  11.5 us (7%)
  other arithmetic  5.86 us (4%)
  local copies, waits for them, and re-layouts  3.18 us (2%)
    all_to_all x1, blocking collectives, body(): lax.all_to_all(new_momentum, 'fsdp', split_axis=0, concat_axis=1, tiled=T...  55.3 us
    all_to_all x1, blocking collectives, body(): lax.all_to_all(iterate, 'fsdp', split_axis=1, concat_axis=0, tiled=True)  53.9 us
    all_gather x1, waiting for transfers between devices, body(): lax.all_gather(jnp.einsum('mik,mjk->mij', moved, moved, precision=HIGH),...  15.9 us
    dot_general x8, matrix products, polynomial(): gram = dot(dot(mixed, gram), mixed)  3.2 us
  transfers between devices with their start and end apart: 1, of which 1 were waited for; matrix products, arithmetic and copies ran while one was open for 0% of the time, Pallas kernels for 0%

profile of v1, /device:TPU:0, one launch (start us, length us, event | category | flops | bytes accessed | tf_op | source)
XLA Modules:
  0.0 159.8 jit_solution(6086261484391665000)
XLA Ops:
  7.2 0.0 all-gather.3.cloned.1.call-start
  7.2 2.7 %multiply_add_fusion = f32[32,16,1024]{2,1,0:T(8,128)S(1)} fusion(f32[32,16,1024]{2,1,0:T(8,128)} %param.3, f32[32,16,1024]{2,1,0:T(8,128)} %param.4), kind=kLoop, calls=%fused_computation.1 | loop fusion | flops 1048576 | bytes 6291456 | tf_op jit(solution)/shard_map/add | solution.py:29
  9.9 0.0 copy-start
  9.9 55.3 %all_to_all.36 = f32[32,16,1024]{2,1,0:T(8,128)S(1)} all-to-all(f32[32,16,1024]{2,1,0:T(8,128)S(1)} %multiply_add_fusion), channel_id=1, replica_groups=mesh['fsdp'=8,'tp'=4] {'fsdp'}, dimensions={0} | all-to-all | bytes 4194304 | tf_op jit(solution)/shard_map/all_to_all | solution.py:30
  65.2 0.0 copy-done
  65.2 0.2 copy.7
  65.4 2.8 %fusion.16 = f32[4,128,128]{2,1,0:T(8,128)} fusion(f32[4,128,1024]{2,1,0:T(8,128)S(1)} %bitcast.44), kind=kOutput, calls=%fused_computation.26 | convolution fusion | flops 805306368 | bytes 2359296 | tf_op jit(solution)/shard_map/mik,mjk->mij/dot_general | solution.py:32
  68.2 0.0 all-gather.3.cloned.1.call-update
  68.3 15.9 %all-gather.3.cloned.1.call-done = f32[16,128,128]{2,1,0:T(8,128)} async-done(((f32[4,128,128]{2,1,0:T(8,128)}), f32[16,128,128]{2,1,0:T(8,128)}) %all-gather.3.cloned.1.call-update) | async-done | bytes 1048592 | tf_op jit(solution)/shard_map/all_gather | solution.py:32
  84.1 1.3 reduce_sum.18
  85.4 0.1 multiply_reduce_fusion
  85.6 0.5 fusion.4
  86.1 0.4 fusion.8
  86.5 0.4 fusion.17
  86.9 0.4 fusion.3
  87.3 0.4 fusion.18
  87.7 0.4 fusion.5
  88.1 0.4 fusion.19
  88.5 0.4 fusion.2
  88.9 0.4 fusion.20
  89.3 0.4 fusion.24
  89.7 0.4 fusion.21
  90.1 0.4 fusion.1
  90.5 0.4 fusion.22
  90.9 0.4 fusion.25
  91.3 0.4 fusion.23
  91.7 0.4 fusion
  92.1 0.4 fusion.26
  92.5 1.9 %fusion.27 = f32[4,128,1024]{2,1,0:T(8,128)S(1)} fusion(f32[4,128,128]{2,1,0:T(8,128)S(1)} %fusion.26, f32[4,128,1024]{2,1,0:T(8,128)S(1)} %bitcast.45), kind=kOutput, calls=%fused_computation.37 | convolution fusion | flops 805306368 | bytes 4456448 | tf_op jit(solution)/shard_map/mij,mjk->mik/dot_general | solution.py:34
  94.4 1.4 copy.8
  95.8 53.9 %all_to_all.37 = f32[4,128,1024]{2,0,1:T(4,128)S(1)} all-to-all(f32[4,128,1024]{2,0,1:T(4,128)S(1)} %copy.8), channel_id=1, replica_groups=mesh['fsdp'=8,'tp'=4] {'fsdp'}, dimensions={1} | all-to-all | bytes 4194304 | tf_op jit(solution)/shard_map/all_to_all | solution.py:35
  149.7 0.0 copy-start.1
  149.7 1.2 copy.9
  150.9 0.4 copy-done.1
  151.3 1.7 %bitcast_subtract_fusion = f32[32,16,1024]{2,1,0:T(8,128)} fusion(f32[32,16,1024]{2,1,0:T(8,128)S(1)} %copy-done.1, f32[8,4,16,1024]{3,2,1,0:T(8,128)S(1)} %copy.9), kind=kLoop, calls=%fused_computation | loop fusion | flops 524288 | bytes 6291456 | tf_op jit(solution)/shard_map/sub | solution.py:36
  (3 shorter events, 0.0 us)
Async XLA Ops:
  7.2 77.0 %all-gather.3.cloned.1.call-start = ((), (), s32[]{:S(2)}) async-start(), calls=%async_computation.2 | async-start | bytes 1310720 | tf_op jit(solution)/shard_map/all_gather | solution.py:32
  9.9 55.3 %copy-start = (f32[32,16,1024]{2,1,0:T(8,128)}, f32[32,16,1024]{2,1,0:T(8,128)S(1)}, u32[]{:S(2)}) copy-start(f32[32,16,1024]{2,1,0:T(8,128)S(1)} %multiply_add_fusion) | copy-start | bytes 6291460
  149.7 1.6 copy-start.1
Sparse Core Ops, SparseCore 0:
  68.3 15.7 all-gather.2
